TPU v7x, 32 devices: a whole 2x2x4 slice. The times are simulated.
32 devices in a mesh: gx: 4 (over z), gy: 4 (over y, x), gz: 2 (over core).
Axes of the slice: x: 2, y: 2, z: 4, core: 2. Of those that a mesh axis runs over, the one named last changes fastest.
Arguments:
- factor_inv: bfloat16 [4, 4096, 2048], P('gx', 'gy', 'gz')
- sep_sizes: int32 [4, 4, 2], P('gx', 'gy', 'gz'), may hold values from 512 to 1024
- coupling: bfloat16 [12, 4096, 2048], P('gx', 'gy', 'gz'), may hold values from -0.109375 to 0.109375
Outputs:
- schur_update: float32 [4, 4096, 2048], P('gx', 'gy', 'gz')
All inputs are finite; a program needn't handle non-finite values.
Results may differ from a plain program's by a relative error of at most 0.0023.
Values may be sent and summed in bfloat16 or wider, within the bound.
A program may use at most 128 MiB of HBM per device.

v0:
```python
import functools

import jax
import jax.numpy as jnp
from jax import lax
from jax.experimental import pallas as pl
from jax.experimental.pallas import tpu as pltpu
from jax.sharding import PartitionSpec as P

MESH = pl.DeviceIdType.MESH
F32, BF16 = jnp.float32, jnp.bfloat16
DIAG = 16
TAIL = 128


def dot(lhs, rhs, left, right):
    return lax.dot_general(lhs, rhs, (((left,), (right,)), ((), ())), preferred_element_type=F32)


def gather_kernel(
    ny, nz, pieces,
    sizes, factor, coupling,
    part_out, tail_out,
    own, couple, beside, solved, total, packed, cross, packed_in, cross_in, full, lows,
    load_sem, z_send, z_recv, y_send, y_recv, store_sem,
):
    width = own.shape[0]
    half = width // 2
    block = half // 2
    steps = width // block
    b, c = lax.axis_index("gy"), lax.axis_index("gz")
    above, below = b < ny - 1, b > 0
    ups, downs = c < nz - 1, c > 0
    peers = ((above, {"gy": b + 1}), (below, {"gy": b - 1}), (ups, {"gz": c + 1}), (downs, {"gz": c - 1}))

    rows_of = [pl.ds(s * block, block) for s in range(steps)]
    factors = [pltpu.make_async_copy(factor.at[0, at], own.at[at], load_sem.at[3 + s]) for s, at in enumerate(rows_of)]
    for load in factors:
        load.start()
    loads = [pltpu.make_async_copy(coupling.at[e], couple.at[e], load_sem.at[e]) for e in range(3)]

    barrier = pltpu.get_barrier_semaphore()
    for there, peer in peers:
        @pl.when(there)
        def _():
            pl.semaphore_signal(barrier, inc=1, device_id=peer, device_id_type=MESH)

    size = sizes[0, 0, 0]
    column = lax.broadcasted_iota(jnp.int32, (1, width), 1) < size
    diag = jnp.zeros((1, width), F32)
    for s in range(steps):
        rows = rows_of[s]
        factors[s].wait()
        row = lax.broadcasted_iota(jnp.int32, (block, 1), 0) + s * block < size
        kept = own[rows, :].astype(F32) * row.astype(F32) * column.astype(F32)
        own[rows, :] = kept.astype(BF16)
        diag = diag + jnp.sum(kept * kept, axis=0, keepdims=True)

    for load in loads:
        load.start()
    pl.semaphore_wait(barrier, sum(there.astype(jnp.int32) for there, _ in peers))

    z_copies = []
    for k, (goes, to, comes) in enumerate(((ups, c + 1, downs), (downs, c - 1, ups))):
        copy = pltpu.make_async_remote_copy(
            src_ref=own, dst_ref=beside.at[k if nz > 2 else 0], send_sem=z_send.at[k], recv_sem=z_recv.at[k],
            device_id={"gz": to}, device_id_type=MESH,
        )
        z_copies.append((goes, comes, copy))

        @pl.when(goes)
        def _():
            copy.start()

    def y_copy(src, dst, k):
        return pltpu.make_async_remote_copy(
            src_ref=src, dst_ref=dst, send_sem=y_send.at[k], recv_sem=y_recv.at[k],
            device_id={"gy": b + 1}, device_id_type=MESH,
        )

    y_copies = [y_copy(packed, packed_in, 0)]
    for k, (start, count) in enumerate(pieces):
        rows = pl.ds(start, count)
        dst = cross_in.at[rows] if k < len(pieces) - 1 else tail_out
        y_copies.append(y_copy(cross.at[rows], dst, k + 1))

    @pl.when(above)
    def _():
        def send_cross(k):
            start, count = pieces[k]
            cross[pl.ds(start, count), :] = dot(own[:, pl.ds(start, count)], own[:, half:], 0, 0).astype(BF16)
            y_copies[k + 1].start()

        send_cross(0)
        line = lax.broadcasted_iota(jnp.int32, (DIAG, half), 0)
        high = diag.astype(BF16).astype(F32)
        low = diag - high
        rows = (high[:, :half], high[:, half:], low[:, :half], low[:, half:])
        lines = jnp.zeros((DIAG, half), F32)
        for i, value in enumerate(rows):
            lines = jnp.where(line == i, value, lines)
        packed[pl.ds(half, DIAG), :] = lines.astype(BF16)
        for s in range(2):
            rows = lax.broadcasted_iota(jnp.int32, (block, half), 0) + s * block
            cols = lax.broadcasted_iota(jnp.int32, (block, half), 1)
            first = dot(own[:, pl.ds(s * block, block)], own[:, :half], 0, 0)
            second = dot(own[:, pl.ds(half + s * block, block)], own[:, half:], 0, 0)
            mixed = jnp.where(rows < cols, first, jnp.where(rows > cols, second, 0.0))
            packed[pl.ds(s * block, block), :] = mixed.astype(BF16)
        y_copies[0].start()
        for k in range(1, len(pieces)):
            send_cross(k)

    for load in loads:
        load.wait()

    def z_slot(slot, k, fresh):
        @pl.loop(0, steps)
        def _(s):
            at = pl.ds(pl.multiple_of(s * block, block), block)
            solved[at, :] = dot(couple[slot, :, at], beside[k], 0, 1).astype(BF16)

        @pl.loop(0, steps)
        def _(s):
            at = pl.ds(pl.multiple_of(s * block, block), block)
            term = dot(solved[at, :], solved[...], 1, 1)
            total[at, :] = term if fresh else total[at, :] + term

    if nz == 2:
        for goes, comes, copy in z_copies:
            @pl.when(comes)
            def _():
                copy.wait_recv()
        z_slot(1 - c, 0, True)
    else:
        total[...] = jnp.zeros_like(total)
        for k, (goes, comes, copy) in enumerate(z_copies):
            @pl.when(comes)
            def _():
                copy.wait_recv()
                z_slot(k, k, False)

    stores = [
        pltpu.make_async_copy(
            total.at[pl.ds(s * block, block)], part_out.at[pl.ds(s * block, block)], store_sem.at[s]
        )
        for s in range(steps)
    ]

    @pl.when(below)
    def _():
        y_copies[0].wait_recv()
        rows = lax.broadcasted_iota(jnp.int32, (half, half), 0)
        cols = lax.broadcasted_iota(jnp.int32, (half, half), 1)
        mixed = packed_in[:half, :].astype(F32)
        lines = packed_in[pl.ds(half, DIAG), :].astype(F32)
        for i, keep in enumerate((rows < cols, rows > cols)):
            one = jnp.where(keep, mixed, 0.0)
            both = one + one.T + jnp.where(rows == cols, lines[i : i + 1, :], 0.0)
            full[i] = both.astype(BF16)
            lows[i] = jnp.where(rows == cols, lines[i + 2 : i + 3, :], 0.0).astype(BF16)

        @pl.loop(0, steps)
        def _(s):
            at = pl.ds(pl.multiple_of(s * block, block), block)
            term = total[at, :]
            for i in range(2):
                piece = couple[2, pl.ds(i * half, half), at]
                high = (dot(piece, full[i], 0, 0) + dot(piece, lows[i], 0, 0)).astype(BF16)
                rest = couple[2, pl.ds(i * half, half), :]
                term = term + dot(high, rest, 1, 0)
            total[at, :] = term

        for k, (start, count) in enumerate(pieces[:-1]):
            y_copies[k + 1].wait_recv()
            rows = pl.ds(start, count)
            high = dot(cross_in[rows, :], couple[2, pl.ds(half, half), :], 1, 0).astype(BF16)
            mine = couple[2, rows, :]
            for i, value in enumerate((mine, high, mine)):
                solved[pl.ds(i * count, count), :] = value
            last = k == len(pieces) - 2
            for s in range(steps):
                at = pl.ds(s * block, block)
                term = dot(solved[pl.ds(0, 2 * count), at], solved[pl.ds(count, 2 * count), :], 0, 0)
                total[at, :] = total[at, :] + term
                if last:
                    stores[s].start()

    @pl.when(jnp.logical_not(below))
    def _():
        for store in stores:
            store.start()

    @pl.when(below)
    def _():
        y_copies[-1].wait_recv()

    for goes, comes, copy in z_copies:
        @pl.when(goes)
        def _():
            copy.wait_send()

    @pl.when(above)
    def _():
        for copy in y_copies:
            copy.wait_send()

    for store in stores:
        store.wait()


def finish_kernel(tail, mine, rest, part, out, left, right):
    count = tail.shape[0]

    @pl.when(pl.program_id(0) == 0)
    def _():
        held = jnp.where(lax.axis_index("gy") > 0, tail[...].astype(F32), 0.0).astype(BF16)
        high = dot(held, rest[0], 1, 0).astype(BF16)
        for i, (one, other) in enumerate(((mine[0], high), (high, mine[0]))):
            left[pl.ds(i * count, count), :] = one
            right[pl.ds(i * count, count), :] = other

    block = out.shape[1]
    at = pl.ds(pl.multiple_of(pl.program_id(0) * block, block), block)
    out[0] = part[...] + dot(left[:, at], right[...], 0, 0)


def on_device(factor_inv, sep_sizes, coupling):
    ny, nz = lax.axis_size("gy"), lax.axis_size("gz")
    width = factor_inv.shape[1]
    inter = coupling.shape[2]
    half = width // 2
    block = half // 2
    steps = width // block
    tail = min(TAIL, block)
    pieces = [(start, tail) for start in range(0, half, tail)]
    count = len(pieces) + 1
    anywhere = pl.BlockSpec(memory_space=pl.ANY)
    part, last = pl.pallas_call(
        functools.partial(gather_kernel, ny, nz, pieces),
        out_shape=(
            jax.ShapeDtypeStruct((inter, inter), F32),
            jax.ShapeDtypeStruct((tail, half), BF16),
        ),
        in_specs=[pl.BlockSpec(memory_space=pltpu.SMEM), anywhere, anywhere],
        out_specs=(anywhere, anywhere),
        scratch_shapes=[
            pltpu.VMEM((width, width), BF16),
            pltpu.VMEM((3, width, inter), BF16),
            pltpu.VMEM((2 if nz > 2 else 1, width, width), BF16),
            pltpu.VMEM((inter, width), BF16),
            pltpu.VMEM((inter, inter), F32),
            pltpu.VMEM((half + DIAG, half), BF16),
            pltpu.VMEM((half, half), BF16),
            pltpu.VMEM((half + DIAG, half), BF16),
            pltpu.VMEM((half, half), BF16),
            pltpu.VMEM((2, half, half), BF16),
            pltpu.VMEM((2, half, half), BF16),
            pltpu.SemaphoreType.DMA((3 + steps,)),
            pltpu.SemaphoreType.DMA((2,)),
            pltpu.SemaphoreType.DMA((2,)),
            pltpu.SemaphoreType.DMA((count,)),
            pltpu.SemaphoreType.DMA((count,)),
            pltpu.SemaphoreType.DMA((steps,)),
        ],
        compiler_params=pltpu.CompilerParams(
            collective_id=0, has_side_effects=True, vmem_limit_bytes=56 * 2**20
        ),
    )(sep_sizes, factor_inv, coupling)
    rows = block
    return pl.pallas_call(
        finish_kernel,
        grid=(inter // rows,),
        out_shape=jax.ShapeDtypeStruct((1, inter, inter), F32),
        in_specs=[
            pl.BlockSpec((tail, half), lambda s: (0, 0)),
            pl.BlockSpec((1, tail, inter), lambda s: (2, half // tail - 1, 0)),
            pl.BlockSpec((1, half, inter), lambda s: (2, 1, 0)),
            pl.BlockSpec((rows, inter), lambda s: (s, 0)),
        ],
        out_specs=pl.BlockSpec((1, rows, inter), lambda s: (0, s, 0)),
        scratch_shapes=[pltpu.VMEM((2 * tail, inter), BF16), pltpu.VMEM((2 * tail, inter), BF16)],
        compiler_params=pltpu.CompilerParams(vmem_limit_bytes=56 * 2**20),
    )(last, coupling, coupling, part)


def solution(mesh):
    return jax.shard_map(
        on_device,
        mesh=mesh,
        in_specs=(P("gx", "gy", "gz"), P("gx", "gy", "gz"), P("gx", "gy", "gz")),
        out_specs=P("gx", "gy", "gz"),
        check_vma=False,
    )
```

profile of v0, /device:TPU:4, one launch (start us, length us, event | category | flops | bytes accessed | tf_op | source)
XLA Modules:
  0.0 37.1 jit_solution(9870028640842697873)
XLA Ops:
  0.7 30.5 %shard_map.37 = (f32[1024,1024]{1,0:T(8,128)}, bf16[128,512]{1,0:T(8,128)(2,1)}) custom-call(s32[1,1,1]{2,1,0:T(1,128)S(6)} %copy.4.sizes, bf16[1,1024,1024]{2,1,0:T(8,128)(2,1)} %factor.1, bf16[3,1024,1024]{2,1,0:T(8,128)(2,1)} %rest.1), custom_call_target="tpu_custom_call" | custom-call | tf_op jit(solution)/shard_map/pallas_call | solution.py:239
  31.1 6.0 %shard_map.38 = f32[1,1024,1024]{2,1,0:T(8,128)} custom-call(bf16[128,512]{1,0:T(8,128)(2,1)} %get-tuple-element.7.tail, bf16[3,1024,1024]{2,1,0:T(8,128)(2,1)} %rest.1, bf16[3,1024,1024]{2,1,0:T(8,128)(2,1)} %rest.1, f32[1024,1024]{1,0:T(8,128)} %get-tuple-element.8.part), custom_call_target="tpu_custom_call" | custom-call | tf_op jit(solution)/shard_map/pallas_call | solution.py:271
where the time goes:
time: 37.3 us; the launch traced here: 37.1 us
  Pallas kernels  36.5 us (98%)
  between operations  0.66 us (2%)
    pallas_call x1, Pallas kernels, on_device(): pl.pallas_call(functools.partial(gather_kernel, ny, nz, pieces), out_shap...  30.5 us
    pallas_call x1, Pallas kernels, on_device(): pl.pallas_call(finish_kernel, grid=(inter // rows,), out_shape=jax.ShapeD...  6 us

commit v1 on v0

v1 whole, which is shorter than its diff:
```python
import functools

import jax
import jax.numpy as jnp
from jax import lax
from jax.experimental import pallas as pl
from jax.experimental.pallas import tpu as pltpu
from jax.sharding import PartitionSpec as P

MESH = pl.DeviceIdType.MESH
F32, BF16 = jnp.float32, jnp.bfloat16
LANES = 128
TAIL = 128


def dot(lhs, rhs, left, right):
    return lax.dot_general(lhs, rhs, (((left,), (right,)), ((), ())), preferred_element_type=F32)


def grid_of(rows, cols):
    return (
        lax.broadcasted_iota(jnp.int32, (rows, cols), 0),
        lax.broadcasted_iota(jnp.int32, (rows, cols), 1),
    )


def gather_kernel(
    ny, nz, pieces,
    sizes, factor, coupling,
    total, mine, tail,
    own, couple, beside, solved, mixed, extra, cross, mixed_in, extra_in, cross_in, full,
    load_sem, z_send, z_recv, y_send, y_recv,
):
    width = own.shape[0]
    half = width // 2
    block = half // 2
    steps = width // block
    per = half // LANES
    b, c = lax.axis_index("gy"), lax.axis_index("gz")
    above, below = b < ny - 1, b > 0
    ups, downs = c < nz - 1, c > 0
    peers = ((above, {"gy": b + 1}), (below, {"gy": b - 1}), (ups, {"gz": c + 1}), (downs, {"gz": c - 1}))

    rows_of = [pl.ds(s * block, block) for s in range(steps)]
    factors = [pltpu.make_async_copy(factor.at[0, at], own.at[at], load_sem.at[3 + s]) for s, at in enumerate(rows_of)]
    for load in factors:
        load.start()

    barrier = pltpu.get_barrier_semaphore()
    for there, peer in peers:
        @pl.when(there)
        def _():
            pl.semaphore_signal(barrier, inc=1, device_id=peer, device_id_type=MESH)

    if nz == 2:
        z_loads = [pltpu.make_async_copy(coupling.at[1 - c], couple.at[0], load_sem.at[0])]
    else:
        z_loads = [pltpu.make_async_copy(coupling.at[e], couple.at[e], load_sem.at[e]) for e in range(2)]
    loads = z_loads + [pltpu.make_async_copy(coupling.at[2], mine, load_sem.at[2])]

    size = sizes[0, 0, 0]
    column = (lax.broadcasted_iota(jnp.int32, (1, width), 1) < size).astype(F32).astype(BF16)
    for s in range(steps):
        rows = rows_of[s]
        row = (lax.broadcasted_iota(jnp.int32, (block, 1), 0) + s * block < size).astype(F32).astype(BF16)
        factors[s].wait()
        own[rows, :] = own[rows, :] * row * column

    for load in loads:
        load.start()

    z_copies = []
    for k, (goes, to, comes) in enumerate(((ups, c + 1, downs), (downs, c - 1, ups))):
        copy = pltpu.make_async_remote_copy(
            src_ref=own, dst_ref=beside.at[k if nz > 2 else 0], send_sem=z_send.at[k], recv_sem=z_recv.at[k],
            device_id={"gz": to}, device_id_type=MESH,
        )
        z_copies.append((goes, comes, copy))

    def y_copy(src, dst, k):
        return pltpu.make_async_remote_copy(
            src_ref=src, dst_ref=dst, send_sem=y_send.at[k], recv_sem=y_recv.at[k],
            device_id={"gy": b + 1}, device_id_type=MESH,
        )

    tops = [pl.ds(s * block, block) for s in range(2)]
    mixes = [y_copy(mixed.at[at], mixed_in.at[at], s) for s, at in enumerate(tops)]
    mixes.append(y_copy(extra, extra_in, 2))
    crosses = []
    for k, (start, count) in enumerate(pieces):
        rows = pl.ds(start, count)
        dst = cross_in.at[rows] if k < len(pieces) - 1 else tail
        crosses.append(y_copy(cross.at[rows], dst, k + 3))

    def make_cross(k):
        start, count = pieces[k]
        cross[pl.ds(start, count), :] = dot(own[:, pl.ds(start, count)], own[:, half:], 0, 0).astype(BF16)

    @pl.when(above)
    def _():
        make_cross(0)

    pl.semaphore_wait(barrier, sum(there.astype(jnp.int32) for there, _ in peers))

    @pl.when(above)
    def _():
        crosses[0].start()

    for goes, comes, copy in z_copies:
        @pl.when(goes)
        def _():
            copy.start()

    @pl.when(above)
    def _():
        r, q = grid_of(block, block)
        lines = []
        first = dot(own[:, :block], own[:, :half], 0, 0)
        second = dot(own[:, half : half + block], own[:, half : half + block], 0, 0)
        mixed[:block, :block] = jnp.where(r <= q, first[:, :block], second).astype(BF16)
        mixed[:block, block:] = first[:, block:].astype(BF16)
        mixes[0].start()
        lines.append((first[:, :block], second))
        second = dot(own[:, half + block :], own[:, half:], 0, 0)
        first = dot(own[:, block:half], own[:, block:half], 0, 0)
        mixed[block:, :block] = second[:, :block].astype(BF16)
        mixed[block:, block:] = jnp.where(r <= q, first, second[:, block:]).astype(BF16)
        mixes[1].start()
        lines.append((first, second[:, block:]))
        at = lax.broadcasted_iota(jnp.int32, extra.shape, 0)
        filled = jnp.zeros(extra.shape, F32)
        for s, pair in enumerate(lines):
            one, two = (jnp.sum(jnp.where(r == q, value, 0.0), axis=0, keepdims=True) for value in pair)
            high = two.astype(BF16).astype(F32)
            for group, line in enumerate((high, one - one.astype(BF16).astype(F32), two - high)):
                for i in range(block // LANES):
                    place = group * per + s * (block // LANES) + i
                    filled = jnp.where(at == place, line[:, i * LANES : (i + 1) * LANES], filled)
        extra[...] = filled.astype(BF16)
        mixes[2].start()
        for k in range(1, len(pieces)):
            make_cross(k)
            crosses[k].start()

    for load in loads:
        load.wait()

    def z_slot(slot, k, fresh):
        @pl.loop(0, steps)
        def _(s):
            at = pl.ds(pl.multiple_of(s * block, block), block)
            solved[at, :] = dot(couple[slot, :, at], beside[k], 0, 1).astype(BF16)

        @pl.loop(0, steps)
        def _(s):
            at = pl.ds(pl.multiple_of(s * block, block), block)
            term = dot(solved[at, :], solved[...], 1, 1)
            total[at, :] = term if fresh else total[at, :] + term

    if nz == 2:
        for goes, comes, copy in z_copies:
            @pl.when(comes)
            def _():
                copy.wait_recv()
        z_slot(0, 0, True)
    else:
        total[...] = jnp.zeros_like(total)
        for k, (goes, comes, copy) in enumerate(z_copies):
            @pl.when(comes)
            def _():
                copy.wait_recv()
                z_slot(k, k, False)

    @pl.when(below)
    def _():
        def use_cross(k):
            start, count = pieces[k]
            crosses[k].wait_recv()
            high = dot(cross_in[pl.ds(start, count), :], mine[half:, :], 1, 0).astype(BF16)
            own_rows = mine[pl.ds(start, count), :]
            for i, value in enumerate((own_rows, high, own_rows)):
                solved[pl.ds(i * count, count), :] = value

            @pl.loop(0, steps)
            def _(s):
                at = pl.ds(pl.multiple_of(s * block, block), block)
                term = dot(solved[pl.ds(0, 2 * count), at], solved[pl.ds(count, 2 * count), :], 0, 0)
                total[at, :] = total[at, :] + term

        use_cross(0)
        for copy in mixes:
            copy.wait_recv()
        r, q = grid_of(half, half)
        value = mixed_in[...].astype(F32)
        turned = value.T
        extras = extra_in[...].astype(F32)

        def line(group):
            return jnp.concatenate([extras[group * per + i : group * per + i + 1, :] for i in range(per)], axis=1)

        full[0] = jnp.where(r <= q, value, turned).astype(BF16)
        full[1] = jnp.where(r > q, value, jnp.where(r == q, line(0), turned)).astype(BF16)
        for i in range(2):
            low = jnp.sum(jnp.where(r == q, line(1 + i), 0.0), axis=1, keepdims=True)
            rows = pl.ds(i * half, half)
            piece = mine[rows, :]
            solved[rows, :] = (dot(full[i], piece, 1, 0) + low * piece.astype(F32)).astype(BF16)

        @pl.loop(0, steps)
        def _(s):
            at = pl.ds(pl.multiple_of(s * block, block), block)
            total[at, :] = total[at, :] + dot(mine[:, at], solved[...], 0, 0)

        for k in range(1, len(pieces) - 1):
            use_cross(k)
        crosses[-1].wait_recv()

    for goes, comes, copy in z_copies:
        @pl.when(goes)
        def _():
            copy.wait_send()

    @pl.when(above)
    def _():
        for copy in mixes + crosses:
            copy.wait_send()


def finish_kernel(total, mine, tail, out, left, right, held, store_sem):
    count, half = tail.shape
    width = total.shape[0]
    last = tail.shape[1] - count
    chunk = TAIL

    kept = jnp.where(lax.axis_index("gy") > 0, tail[...].astype(F32), 0.0).astype(BF16)
    high = dot(kept, mine[half:, :], 1, 0).astype(BF16)
    rows = mine[pl.ds(last, count), :]
    for i, (one, other) in enumerate(((rows, high), (high, rows))):
        left[pl.ds(i * count, count), :] = one
        right[pl.ds(i * count, count), :] = other
    stores = []
    for s in range(width // chunk):
        at = pl.ds(s * chunk, chunk)
        held[at, :] = total[at, :] + dot(left[:, at], right[...], 0, 0)
        store = pltpu.make_async_copy(held.at[at], out.at[0, at], store_sem.at[s])
        store.start()
        stores.append(store)
    for store in stores:
        store.wait()


def in_place(array):
    return pltpu.with_memory_space_constraint(array, pltpu.HBM)


def on_device(factor_inv, sep_sizes, coupling):
    ny, nz = lax.axis_size("gy"), lax.axis_size("gz")
    width = factor_inv.shape[1]
    inter = coupling.shape[2]
    half = width // 2
    block = half // 2
    steps = width // block
    sides = 2 if nz > 2 else 1
    tail = min(TAIL, block)
    pieces = [(start, tail) for start in range(0, half, tail)]
    count = len(pieces) + 3
    extra = (-(-3 * (half // LANES) // 16) * 16, LANES)
    anywhere = pl.BlockSpec(memory_space=pl.ANY)
    inside = pl.BlockSpec(memory_space=pltpu.VMEM)
    total, mine, last = pl.pallas_call(
        functools.partial(gather_kernel, ny, nz, pieces),
        out_shape=(
            pltpu.VMEM((inter, inter), F32),
            pltpu.VMEM((width, inter), BF16),
            pltpu.VMEM((tail, half), BF16),
        ),
        in_specs=[pl.BlockSpec(memory_space=pltpu.SMEM), anywhere, anywhere],
        out_specs=(inside, inside, inside),
        scratch_shapes=[
            pltpu.VMEM((width, width), BF16),
            pltpu.VMEM((sides, width, inter), BF16),
            pltpu.VMEM((sides, width, width), BF16),
            pltpu.VMEM((inter, width), BF16),
            pltpu.VMEM((half, half), BF16),
            pltpu.VMEM(extra, BF16),
            pltpu.VMEM((half, half), BF16),
            pltpu.VMEM((half, half), BF16),
            pltpu.VMEM(extra, BF16),
            pltpu.VMEM((half, half), BF16),
            pltpu.VMEM((2, half, half), BF16),
            pltpu.SemaphoreType.DMA((3 + steps,)),
            pltpu.SemaphoreType.DMA((2,)),
            pltpu.SemaphoreType.DMA((2,)),
            pltpu.SemaphoreType.DMA((count,)),
            pltpu.SemaphoreType.DMA((count,)),
        ],
        compiler_params=pltpu.CompilerParams(
            collective_id=0, has_side_effects=True, vmem_limit_bytes=40 * 2**20
        ),
    )(sep_sizes, in_place(factor_inv), in_place(coupling))
    return pl.pallas_call(
        finish_kernel,
        out_shape=jax.ShapeDtypeStruct((1, inter, inter), F32),
        in_specs=[inside, inside, inside],
        out_specs=anywhere,
        scratch_shapes=[
            pltpu.VMEM((2 * tail, inter), BF16),
            pltpu.VMEM((2 * tail, inter), BF16),
            pltpu.VMEM((inter, inter), F32),
            pltpu.SemaphoreType.DMA((inter // TAIL,)),
        ],
        compiler_params=pltpu.CompilerParams(vmem_limit_bytes=40 * 2**20),
    )(total, mine, last)


def solution(mesh):
    return jax.shard_map(
        on_device,
        mesh=mesh,
        in_specs=(P("gx", "gy", "gz"), P("gx", "gy", "gz"), P("gx", "gy", "gz")),
        out_specs=P("gx", "gy", "gz"),
        check_vma=False,
    )
```

time: 37.3 us -> 30.4 us (0.82)
  Pallas kernels: 36.5 us -> 29.6 us
    pallas_call x1, Pallas kernels: 30.5 us -> 27 us  [on_device(): pl.pallas_call(functools.partial(gather_kernel, ny, nz, pieces), out_shap...]
    pallas_call x1, Pallas kernels: 6 us -> 2.6 us  [on_device(): pl.pallas_call(finish_kernel, out_shape=jax.ShapeDtypeStruct((1, inter, i...]
where the time goes in v1:
time: 30.4 us; the launch traced here: 30.3 us
  Pallas kernels  29.6 us (97%)
  between operations  0.66 us (2%)
    pallas_call x1, Pallas kernels, on_device(): pl.pallas_call(functools.partial(gather_kernel, ny, nz, pieces), out_shap...  27 us
    pallas_call x1, Pallas kernels, on_device(): pl.pallas_call(finish_kernel, out_shape=jax.ShapeDtypeStruct((1, inter, i...  2.6 us

profile of v1, /device:TPU:4, one launch (start us, length us, event | category | flops | bytes accessed | tf_op | source)
XLA Modules:
  0.0 30.3 jit_solution(11619948956700548971)
XLA Ops:
  0.7 27.0 %shard_map.37 = (f32[1024,1024]{1,0:T(8,128)S(1)}, bf16[1024,1024]{1,0:T(8,128)(2,1)S(1)}, bf16[128,512]{1,0:T(8,128)(2,1)S(1)}) custom-call(s32[1,1,1]{2,1,0:T(1,128)S(6)} %copy.4.sizes, bf16[1,1024,1024]{2,1,0:T(8,128)(2,1)} %factor.1, bf16[3,1024,1024]{2,1,0:T(8,128)(2,1)} %coupling.1), custom_call_target="tpu_custom_call" | custom-call | tf_op jit(solution)/shard_map/pallas_call | solution.py:270
  27.7 2.6 %shard_map.38 = f32[1,1024,1024]{2,1,0:T(8,128)} custom-call(f32[1024,1024]{1,0:T(8,128)S(1)} %get-tuple-element.8.total, bf16[1024,1024]{1,0:T(8,128)(2,1)S(1)} %get-tuple-element.9.mine, bf16[128,512]{1,0:T(8,128)(2,1)S(1)} %get-tuple-element.10.tail), custom_call_target="tpu_custom_call" | custom-call | tf_op jit(solution)/shard_map/pallas_call | solution.py:301

commit v2 on v1

--- a/solution.py
+++ b/solution.py
@@ -11,6 +11,7 @@
 F32, BF16 = jnp.float32, jnp.bfloat16
 LANES = 128
 TAIL = 128
+RELAYED = 1
 
 
 def dot(lhs, rhs, left, right):
@@ -25,11 +26,11 @@
 
 
 def gather_kernel(
-    ny, nz, pieces,
+    ny, nz, pieces, relay,
     sizes, factor, coupling,
     total, mine, tail,
-    own, couple, beside, solved, mixed, extra, cross, mixed_in, extra_in, cross_in, full,
-    load_sem, z_send, z_recv, y_send, y_recv,
+    own, couple, beside, solved, mixed, extra, cross, mixed_in, extra_in, cross_in, full, passed,
+    load_sem, z_send, z_recv, y_send, y_recv, pass_send, pass_recv,
 ):
     width = own.shape[0]
     half = width // 2
@@ -39,7 +40,12 @@
     b, c = lax.axis_index("gy"), lax.axis_index("gz")
     above, below = b < ny - 1, b > 0
     ups, downs = c < nz - 1, c > 0
-    peers = ((above, {"gy": b + 1}), (below, {"gy": b - 1}), (ups, {"gz": c + 1}), (downs, {"gz": c - 1}))
+    greets = [(below, {"gy": b - 1}), (ups, {"gz": c + 1}), (downs, {"gz": c - 1})]
+    awaits = [above, ups, downs]
+    if relay is not None:
+        far, via = relay
+        greets = [(b == via, {"gy": far})] + greets + [(b == far + 1, {"gy": via})]
+        awaits += [b == far, b == via]
 
     rows_of = [pl.ds(s * block, block) for s in range(steps)]
     factors = [pltpu.make_async_copy(factor.at[0, at], own.at[at], load_sem.at[3 + s]) for s, at in enumerate(rows_of)]
@@ -47,7 +53,7 @@
         load.start()
 
     barrier = pltpu.get_barrier_semaphore()
-    for there, peer in peers:
+    for there, peer in greets:
         @pl.when(there)
         def _():
             pl.semaphore_signal(barrier, inc=1, device_id=peer, device_id_type=MESH)
@@ -92,6 +98,32 @@
         dst = cross_in.at[rows] if k < len(pieces) - 1 else tail
         crosses.append(y_copy(cross.at[rows], dst, k + 3))
 
+    first_hop = second_hop = None
+    if relay is not None:
+        start, count = pieces[RELAYED]
+        first_hop = pltpu.make_async_remote_copy(
+            src_ref=cross.at[pl.ds(start, count)], dst_ref=passed,
+            send_sem=y_send.at[RELAYED + 3], recv_sem=pass_recv.at[0],
+            device_id={"gy": via}, device_id_type=MESH,
+        )
+        second_hop = pltpu.make_async_remote_copy(
+            src_ref=passed, dst_ref=cross_in.at[pl.ds(start, count)],
+            send_sem=pass_send.at[0], recv_sem=y_recv.at[RELAYED + 3],
+            device_id={"gy": far + 1}, device_id_type=MESH,
+        )
+
+    def send_cross(k):
+        if relay is None or k != RELAYED:
+            crosses[k].start()
+        else:
+            @pl.when(b == far)
+            def _():
+                first_hop.start()
+
+            @pl.when(b != far)
+            def _():
+                crosses[k].start()
+
     def make_cross(k):
         start, count = pieces[k]
         cross[pl.ds(start, count), :] = dot(own[:, pl.ds(start, count)], own[:, half:], 0, 0).astype(BF16)
@@ -100,7 +132,7 @@
     def _():
         make_cross(0)
 
-    pl.semaphore_wait(barrier, sum(there.astype(jnp.int32) for there, _ in peers))
+    pl.semaphore_wait(barrier, sum(there.astype(jnp.int32) for there in awaits))
 
     @pl.when(above)
     def _():
@@ -140,22 +172,21 @@
         mixes[2].start()
         for k in range(1, len(pieces)):
             make_cross(k)
-            crosses[k].start()
+            send_cross(k)
+
+    if relay is not None:
+        @pl.when(b == via)
+        def _():
+            first_hop.wait_recv()
+            second_hop.start()
 
     for load in loads:
         load.wait()
 
     def z_slot(slot, k, fresh):
-        @pl.loop(0, steps)
-        def _(s):
-            at = pl.ds(pl.multiple_of(s * block, block), block)
-            solved[at, :] = dot(couple[slot, :, at], beside[k], 0, 1).astype(BF16)
-
-        @pl.loop(0, steps)
-        def _(s):
-            at = pl.ds(pl.multiple_of(s * block, block), block)
-            term = dot(solved[at, :], solved[...], 1, 1)
-            total[at, :] = term if fresh else total[at, :] + term
+        solved[...] = dot(beside[k], couple[slot], 1, 0).astype(BF16)
+        term = dot(solved[...], solved[...], 0, 0)
+        total[...] = term if fresh else total[...] + term
 
     if nz == 2:
         for goes, comes, copy in z_copies:
@@ -171,6 +202,7 @@
                 copy.wait_recv()
                 z_slot(k, k, False)
 
+
     @pl.when(below)
     def _():
         def use_cross(k):
@@ -181,11 +213,7 @@
             for i, value in enumerate((own_rows, high, own_rows)):
                 solved[pl.ds(i * count, count), :] = value
 
-            @pl.loop(0, steps)
-            def _(s):
-                at = pl.ds(pl.multiple_of(s * block, block), block)
-                term = dot(solved[pl.ds(0, 2 * count), at], solved[pl.ds(count, 2 * count), :], 0, 0)
-                total[at, :] = total[at, :] + term
+            total[...] = total[...] + dot(solved[pl.ds(0, 2 * count), :], solved[pl.ds(count, 2 * count), :], 0, 0)
 
         use_cross(0)
         for copy in mixes:
@@ -206,10 +234,7 @@
             piece = mine[rows, :]
             solved[rows, :] = (dot(full[i], piece, 1, 0) + low * piece.astype(F32)).astype(BF16)
 
-        @pl.loop(0, steps)
-        def _(s):
-            at = pl.ds(pl.multiple_of(s * block, block), block)
-            total[at, :] = total[at, :] + dot(mine[:, at], solved[...], 0, 0)
+        total[...] = total[...] + dot(mine[...], solved[...], 0, 0)
 
         for k in range(1, len(pieces) - 1):
             use_cross(k)
@@ -224,6 +249,11 @@
     def _():
         for copy in mixes + crosses:
             copy.wait_send()
+
+    if relay is not None:
+        @pl.when(b == via)
+        def _():
+            second_hop.wait_send()
 
 
 def finish_kernel(total, mine, tail, out, left, right, held, store_sem):
@@ -253,7 +283,7 @@
     return pltpu.with_memory_space_constraint(array, pltpu.HBM)
 
 
-def on_device(factor_inv, sep_sizes, coupling):
+def on_device(relay, factor_inv, sep_sizes, coupling):
     ny, nz = lax.axis_size("gy"), lax.axis_size("gz")
     width = factor_inv.shape[1]
     inter = coupling.shape[2]
@@ -268,7 +298,7 @@
     anywhere = pl.BlockSpec(memory_space=pl.ANY)
     inside = pl.BlockSpec(memory_space=pltpu.VMEM)
     total, mine, last = pl.pallas_call(
-        functools.partial(gather_kernel, ny, nz, pieces),
+        functools.partial(gather_kernel, ny, nz, pieces, relay),
         out_shape=(
             pltpu.VMEM((inter, inter), F32),
             pltpu.VMEM((width, inter), BF16),
@@ -280,7 +310,7 @@
             pltpu.VMEM((width, width), BF16),
             pltpu.VMEM((sides, width, inter), BF16),
             pltpu.VMEM((sides, width, width), BF16),
-            pltpu.VMEM((inter, width), BF16),
+            pltpu.VMEM((width, inter), BF16),
             pltpu.VMEM((half, half), BF16),
             pltpu.VMEM(extra, BF16),
             pltpu.VMEM((half, half), BF16),
@@ -288,11 +318,14 @@
             pltpu.VMEM(extra, BF16),
             pltpu.VMEM((half, half), BF16),
             pltpu.VMEM((2, half, half), BF16),
+            pltpu.VMEM((pieces[RELAYED][1], half), BF16),
             pltpu.SemaphoreType.DMA((3 + steps,)),
             pltpu.SemaphoreType.DMA((2,)),
             pltpu.SemaphoreType.DMA((2,)),
             pltpu.SemaphoreType.DMA((count,)),
             pltpu.SemaphoreType.DMA((count,)),
+            pltpu.SemaphoreType.DMA((1,)),
+            pltpu.SemaphoreType.DMA((1,)),
         ],
         compiler_params=pltpu.CompilerParams(
             collective_id=0, has_side_effects=True, vmem_limit_bytes=40 * 2**20
@@ -313,9 +346,24 @@
     )(total, mine, last)
 
 
+def relay_of(mesh):
+    line = [getattr(mesh.devices[0, b, 0], "coords", None) for b in range(mesh.shape["gy"])]
+    if any(at is None for at in line):
+        return None
+    for b in range(len(line) - 1):
+        here, there = line[b], line[b + 1]
+        apart = [i for i in range(len(here)) if here[i] != there[i]]
+        if len(apart) == 2 and all(abs(here[i] - there[i]) == 1 for i in apart):
+            corner = list(here)
+            corner[apart[1]] = there[apart[1]]
+            if list(corner) in [list(at) for at in line]:
+                return b, [list(at) for at in line].index(list(corner))
+    return None
+
+
 def solution(mesh):
     return jax.shard_map(
-        on_device,
+        functools.partial(on_device, relay_of(mesh)),
         mesh=mesh,
         in_specs=(P("gx", "gy", "gz"), P("gx", "gy", "gz"), P("gx", "gy", "gz")),
         out_specs=P("gx", "gy", "gz"),

time: 30.4 us -> 29.4 us (0.967)
  the two profiles are of different devices: /device:TPU:4 before, /device:TPU:0 now
where the time goes in v2:
time: 29.4 us; the launch traced here: 29 us
  Pallas kernels  28.3 us (96%)
  between operations  0.66 us (2%)
    pallas_call x1, Pallas kernels, on_device(): pl.pallas_call(functools.partial(gather_kernel, ny, nz, pieces, relay), o...  25.7 us
    pallas_call x1, Pallas kernels, on_device(): pl.pallas_call(finish_kernel, out_shape=jax.ShapeDtypeStruct((1, inter, i...  2.6 us

profile of v2, /device:TPU:0, one launch (start us, length us, event | category | flops | bytes accessed | tf_op | source)
XLA Modules:
  0.0 29.0 jit_solution(3753414212888032096)
XLA Ops:
  0.7 25.7 %shard_map.37 = (f32[1024,1024]{1,0:T(8,128)S(1)}, bf16[1024,1024]{1,0:T(8,128)(2,1)S(1)}, bf16[128,512]{1,0:T(8,128)(2,1)S(1)}) custom-call(s32[1,1,1]{2,1,0:T(1,128)S(6)} %copy.4.sizes, bf16[1,1024,1024]{2,1,0:T(8,128)(2,1)} %factor.1, bf16[3,1024,1024]{2,1,0:T(8,128)(2,1)} %coupling.1), custom_call_target="tpu_custom_call" | custom-call | tf_op jit(solution)/shard_map/pallas_call | solution.py:300
  26.4 2.6 %shard_map.38 = f32[1,1024,1024]{2,1,0:T(8,128)} custom-call(f32[1024,1024]{1,0:T(8,128)S(1)} %get-tuple-element.8.total, bf16[1024,1024]{1,0:T(8,128)(2,1)S(1)} %get-tuple-element.9.mine, bf16[128,512]{1,0:T(8,128)(2,1)S(1)} %get-tuple-element.10.tail), custom_call_target="tpu_custom_call" | custom-call | tf_op jit(solution)/shard_map/pallas_call | solution.py:334

commit v3 on v2

--- a/solution.py
+++ b/solution.py
@@ -11,6 +11,8 @@
 F32, BF16 = jnp.float32, jnp.bfloat16
 LANES = 128
 TAIL = 128
+TIP = 128
+LATE = 32
 RELAYED = 1
 
 
@@ -28,7 +30,7 @@
 def gather_kernel(
     ny, nz, pieces, relay,
     sizes, factor, coupling,
-    total, mine, tail,
+    total, mine, tail, ready,
     own, couple, beside, solved, mixed, extra, cross, mixed_in, extra_in, cross_in, full, passed,
     load_sem, z_send, z_recv, y_send, y_recv, pass_send, pass_recv,
 ):
@@ -47,17 +49,18 @@
         greets = [(b == via, {"gy": far})] + greets + [(b == far + 1, {"gy": via})]
         awaits += [b == far, b == via]
 
-    rows_of = [pl.ds(s * block, block) for s in range(steps)]
-    factors = [pltpu.make_async_copy(factor.at[0, at], own.at[at], load_sem.at[3 + s]) for s, at in enumerate(rows_of)]
-    for load in factors:
-        load.start()
-
     barrier = pltpu.get_barrier_semaphore()
     for there, peer in greets:
         @pl.when(there)
         def _():
             pl.semaphore_signal(barrier, inc=1, device_id=peer, device_id_type=MESH)
 
+    spans = ((0, TIP), (half, half + TIP), (TIP, half), (half + TIP, width))
+    parts = [pl.ds(start, end - start) for start, end in spans]
+    factors = [pltpu.make_async_copy(factor.at[0, :, at], own.at[:, at], load_sem.at[3 + s]) for s, at in enumerate(parts)]
+    for load in factors:
+        load.start()
+
     if nz == 2:
         z_loads = [pltpu.make_async_copy(coupling.at[1 - c], couple.at[0], load_sem.at[0])]
     else:
@@ -65,15 +68,22 @@
     loads = z_loads + [pltpu.make_async_copy(coupling.at[2], mine, load_sem.at[2])]
 
     size = sizes[0, 0, 0]
-    column = (lax.broadcasted_iota(jnp.int32, (1, width), 1) < size).astype(F32).astype(BF16)
-    for s in range(steps):
-        rows = rows_of[s]
-        row = (lax.broadcasted_iota(jnp.int32, (block, 1), 0) + s * block < size).astype(F32).astype(BF16)
+    row = (lax.broadcasted_iota(jnp.int32, (width, 1), 0) < size).astype(F32).astype(BF16)
+
+    def mask(s):
+        start, end = spans[s]
+        column = (lax.broadcasted_iota(jnp.int32, (1, end - start), 1) + start < size).astype(F32).astype(BF16)
         factors[s].wait()
-        own[rows, :] = own[rows, :] * row * column
-
-    for load in loads:
-        load.start()
+        own[:, parts[s]] = own[:, parts[s]] * row * column
+
+    mask(0)
+    mask(1)
+
+    @pl.when(above)
+    def _():
+        tip = dot(own[:, :TIP], own[:, half : half + TIP], 0, 0)
+        cross[:TIP, :TIP] = tip.astype(BF16)
+
 
     z_copies = []
     for k, (goes, to, comes) in enumerate(((ups, c + 1, downs), (downs, c - 1, ups))):
@@ -96,7 +106,11 @@
     for k, (start, count) in enumerate(pieces):
         rows = pl.ds(start, count)
         dst = cross_in.at[rows] if k < len(pieces) - 1 else tail
-        crosses.append(y_copy(cross.at[rows], dst, k + 3))
+        if k == 0:
+            crosses.append(y_copy(cross.at[rows, pl.ds(TIP, half - TIP)], cross_in.at[rows, pl.ds(TIP, half - TIP)], 3))
+        else:
+            crosses.append(y_copy(cross.at[rows], dst, k + 3))
+    crosses.append(y_copy(cross.at[pl.ds(0, TIP), pl.ds(0, TIP)], cross_in.at[pl.ds(0, TIP), pl.ds(0, TIP)], len(pieces) + 3))
 
     first_hop = second_hop = None
     if relay is not None:
@@ -128,14 +142,21 @@
         start, count = pieces[k]
         cross[pl.ds(start, count), :] = dot(own[:, pl.ds(start, count)], own[:, half:], 0, 0).astype(BF16)
 
+    pl.semaphore_wait(barrier, sum(there.astype(jnp.int32) for there in awaits))
+
     @pl.when(above)
     def _():
-        make_cross(0)
-
-    pl.semaphore_wait(barrier, sum(there.astype(jnp.int32) for there in awaits))
+        crosses[-1].start()
+
+    mask(2)
+    mask(3)
+    for load in loads:
+        load.start()
 
     @pl.when(above)
     def _():
+        edge = dot(own[:, :TIP], own[:, half + TIP :], 0, 0)
+        cross[:TIP, TIP:] = edge.astype(BF16)
         crosses[0].start()
 
     for goes, comes, copy in z_copies:
@@ -208,6 +229,8 @@
         def use_cross(k):
             start, count = pieces[k]
             crosses[k].wait_recv()
+            if k == 0:
+                crosses[-1].wait_recv()
             high = dot(cross_in[pl.ds(start, count), :], mine[half:, :], 1, 0).astype(BF16)
             own_rows = mine[pl.ds(start, count), :]
             for i, value in enumerate((own_rows, high, own_rows)):
@@ -236,9 +259,16 @@
 
         total[...] = total[...] + dot(mine[...], solved[...], 0, 0)
 
-        for k in range(1, len(pieces) - 1):
+        for k in range(1, len(pieces) - 2):
             use_cross(k)
-        crosses[-1].wait_recv()
+        start, count = pieces[-2]
+        crosses[-3].wait_recv()
+        ready[...] = dot(cross_in[pl.ds(start, count), :], mine[half:, :], 1, 0).astype(BF16)
+        crosses[-2].wait_recv()
+
+    @pl.when(jnp.logical_not(below))
+    def _():
+        ready[...] = jnp.zeros_like(ready)
 
     for goes, comes, copy in z_copies:
         @pl.when(goes)
@@ -256,18 +286,22 @@
             second_hop.wait_send()
 
 
-def finish_kernel(total, mine, tail, out, left, right, held, store_sem):
-    count, half = tail.shape
+def finish_kernel(total, mine, tail, ready, out, left, right, held, store_sem):
+    late, half = tail.shape
+    early = ready.shape[0]
+    count = early + late
     width = total.shape[0]
-    last = tail.shape[1] - count
     chunk = TAIL
 
     kept = jnp.where(lax.axis_index("gy") > 0, tail[...].astype(F32), 0.0).astype(BF16)
+    rows = mine[pl.ds(half - count, count), :]
+    left[:count, :] = rows
+    right[count:, :] = rows
+    left[count : count + early, :] = ready[...]
+    right[:early, :] = ready[...]
     high = dot(kept, mine[half:, :], 1, 0).astype(BF16)
-    rows = mine[pl.ds(last, count), :]
-    for i, (one, other) in enumerate(((rows, high), (high, rows))):
-        left[pl.ds(i * count, count), :] = one
-        right[pl.ds(i * count, count), :] = other
+    left[count + early :, :] = high
+    right[early:count, :] = high
     stores = []
     for s in range(width // chunk):
         at = pl.ds(s * chunk, chunk)
@@ -293,19 +327,22 @@
     sides = 2 if nz > 2 else 1
     tail = min(TAIL, block)
     pieces = [(start, tail) for start in range(0, half, tail)]
-    count = len(pieces) + 3
+    early = tail - LATE
+    pieces = pieces[:-1] + [(half - tail, early), (half - LATE, LATE)]
+    count = len(pieces) + 4
     extra = (-(-3 * (half // LANES) // 16) * 16, LANES)
     anywhere = pl.BlockSpec(memory_space=pl.ANY)
     inside = pl.BlockSpec(memory_space=pltpu.VMEM)
-    total, mine, last = pl.pallas_call(
+    total, mine, last, ready = pl.pallas_call(
         functools.partial(gather_kernel, ny, nz, pieces, relay),
         out_shape=(
             pltpu.VMEM((inter, inter), F32),
             pltpu.VMEM((width, inter), BF16),
-            pltpu.VMEM((tail, half), BF16),
+            pltpu.VMEM((LATE, half), BF16),
+            pltpu.VMEM((early, inter), BF16),
         ),
         in_specs=[pl.BlockSpec(memory_space=pltpu.SMEM), anywhere, anywhere],
-        out_specs=(inside, inside, inside),
+        out_specs=(inside,) * 4,
         scratch_shapes=[
             pltpu.VMEM((width, width), BF16),
             pltpu.VMEM((sides, width, inter), BF16),
@@ -319,7 +356,7 @@
             pltpu.VMEM((half, half), BF16),
             pltpu.VMEM((2, half, half), BF16),
             pltpu.VMEM((pieces[RELAYED][1], half), BF16),
-            pltpu.SemaphoreType.DMA((3 + steps,)),
+            pltpu.SemaphoreType.DMA((7,)),
             pltpu.SemaphoreType.DMA((2,)),
             pltpu.SemaphoreType.DMA((2,)),
             pltpu.SemaphoreType.DMA((count,)),
@@ -334,7 +371,7 @@
     return pl.pallas_call(
         finish_kernel,
         out_shape=jax.ShapeDtypeStruct((1, inter, inter), F32),
-        in_specs=[inside, inside, inside],
+        in_specs=[inside] * 4,
         out_specs=anywhere,
         scratch_shapes=[
             pltpu.VMEM((2 * tail, inter), BF16),
@@ -343,7 +380,7 @@
             pltpu.SemaphoreType.DMA((inter // TAIL,)),
         ],
         compiler_params=pltpu.CompilerParams(vmem_limit_bytes=40 * 2**20),
-    )(total, mine, last)
+    )(total, mine, last, ready)
 
 
 def relay_of(mesh):

time: 29.4 us -> 29.3 us (level)
  no operation moved by 1% of the time
where the time goes in v3:
time: 29.3 us; the launch traced here: 29.2 us
  Pallas kernels  28.5 us (97%)
  between operations  0.66 us (2%)
    pallas_call x1, Pallas kernels, on_device(): pl.pallas_call(functools.partial(gather_kernel, ny, nz, pieces, relay), o...  26 us
    pallas_call x1, Pallas kernels, on_device(): pl.pallas_call(finish_kernel, out_shape=jax.ShapeDtypeStruct((1, inter, i...  2.55 us

profile of v3, /device:TPU:0, one launch (start us, length us, event | category | flops | bytes accessed | tf_op | source)
XLA Modules:
  0.0 29.2 jit_solution(7822969375274285220)
XLA Ops:
  0.7 26.0 %shard_map.37 = (f32[1024,1024]{1,0:T(8,128)S(1)}, bf16[1024,1024]{1,0:T(8,128)(2,1)S(1)}, bf16[32,512]{1,0:T(8,128)(2,1)S(1)}, bf16[96,1024]{1,0:T(8,128)(2,1)S(1)}) custom-call(s32[1,1,1]{2,1,0:T(1,128)S(6)} %copy.4.sizes, bf16[1,1024,1024]{2,1,0:T(8,128)(2,1)} %factor.1, bf16[3,1024,1024]{2,1,0:T(8,128)(2,1)} %coupling.1), custom_call_target="tpu_custom_call" | custom-call | tf_op jit(solution)/shard_map/pallas_call | solution.py:336
  26.6 2.6 %shard_map.38 = f32[1,1024,1024]{2,1,0:T(8,128)} custom-call(f32[1024,1024]{1,0:T(8,128)S(1)} %get-tuple-element.9.total, bf16[1024,1024]{1,0:T(8,128)(2,1)S(1)} %get-tuple-element.10.mine, bf16[32,512]{1,0:T(8,128)(2,1)S(1)} %get-tuple-element.11.tail, bf16[96,1024]{1,0:T(8,128)(2,1)S(1)} %get-tuple-element.12.ready), custom_call_target="tpu_custom_call" | custom-call | tf_op jit(solution)/shard_map/pallas_call | solution.py:371

commit v4 on v3

--- a/solution.py
+++ b/solution.py
@@ -46,7 +46,7 @@
     awaits = [above, ups, downs]
     if relay is not None:
         far, via = relay
-        greets = [(b == via, {"gy": far})] + greets + [(b == far + 1, {"gy": via})]
+        greets += [(b == via, {"gy": far}), (b == far + 1, {"gy": via})]
         awaits += [b == far, b == via]
 
     barrier = pltpu.get_barrier_semaphore()
@@ -142,16 +142,16 @@
         start, count = pieces[k]
         cross[pl.ds(start, count), :] = dot(own[:, pl.ds(start, count)], own[:, half:], 0, 0).astype(BF16)
 
-    pl.semaphore_wait(barrier, sum(there.astype(jnp.int32) for there in awaits))
-
-    @pl.when(above)
-    def _():
-        crosses[-1].start()
-
     mask(2)
     mask(3)
     for load in loads:
         load.start()
+
+    pl.semaphore_wait(barrier, sum(there.astype(jnp.int32) for there in awaits))
+
+    @pl.when(above)
+    def _():
+        crosses[-1].start()
 
     @pl.when(above)
     def _():

time: 29.3 us -> 29.1 us (level)
  no operation moved by 1% of the time
where the time goes in v4:
time: 29.1 us; the launch traced here: 29 us
  Pallas kernels  28.3 us (97%)
  between operations  0.66 us (2%)
    pallas_call x1, Pallas kernels, on_device(): pl.pallas_call(functools.partial(gather_kernel, ny, nz, pieces, relay), o...  25.8 us
    pallas_call x1, Pallas kernels, on_device(): pl.pallas_call(finish_kernel, out_shape=jax.ShapeDtypeStruct((1, inter, i...  2.56 us

profile of v4, /device:TPU:0, one launch (start us, length us, event | category | flops | bytes accessed | tf_op | source)
XLA Modules:
  0.0 29.0 jit_solution(5891740025682095512)
XLA Ops:
  0.7 25.8 %shard_map.37 = (f32[1024,1024]{1,0:T(8,128)S(1)}, bf16[1024,1024]{1,0:T(8,128)(2,1)S(1)}, bf16[32,512]{1,0:T(8,128)(2,1)S(1)}, bf16[96,1024]{1,0:T(8,128)(2,1)S(1)}) custom-call(s32[1,1,1]{2,1,0:T(1,128)S(6)} %copy.4.sizes, bf16[1,1024,1024]{2,1,0:T(8,128)(2,1)} %factor.1, bf16[3,1024,1024]{2,1,0:T(8,128)(2,1)} %coupling.1), custom_call_target="tpu_custom_call" | custom-call | tf_op jit(solution)/shard_map/pallas_call | solution.py:336
  26.4 2.6 %shard_map.38 = f32[1,1024,1024]{2,1,0:T(8,128)} custom-call(f32[1024,1024]{1,0:T(8,128)S(1)} %get-tuple-element.9.total, bf16[1024,1024]{1,0:T(8,128)(2,1)S(1)} %get-tuple-element.10.mine, bf16[32,512]{1,0:T(8,128)(2,1)S(1)} %get-tuple-element.11.tail, bf16[96,1024]{1,0:T(8,128)(2,1)S(1)} %get-tuple-element.12.ready), custom_call_target="tpu_custom_call" | custom-call | tf_op jit(solution)/shard_map/pallas_call | solution.py:371
